TPU v7x, 128 devices: a whole 4x4x4 slice. The times are simulated.
128 devices in a mesh: row: 8 (over x, core), col: 16 (over z, y).
Axes of the slice: x: 4, y: 4, z: 4, core: 2. Of those that a mesh axis runs over, the one named last changes fastest.
Arguments:
- velocity: float32 [3, 32, 2048, 1024], P(None, None, 'col', 'row'), may hold values from -6 to 6
- z_inverse: float32 [1024, 1024], replicated, may hold values from -0.1875 to 0.1875
- tiles: int32 [1024, 4], P(('row', 'col')), may hold values from 0 to 8191, as said below
- amplitude: float32 [1024, 4, 256], P(('row', 'col')), may hold values from -3 to 3
- lateral: float32 [1024, 8, 256], P(('row', 'col')), may hold values from -2 to 2
- vertical: float32 [1024, 128, 256], P(('row', 'col')), may hold values from -0.5 to 0.5
- wall_velocity: float32 [1024, 3, 256], P(('row', 'col')), may hold values from -6 to 6
- surface: float32 [1024, 256], P(('row', 'col')), may hold values from 0.5 to 2
Outputs:
- spectrum: float32 [2, 3, 32, 1024, 1024], P(None, None, 'row', 'col')
- marker_force: float32 [1024, 3, 256], P(('row', 'col'))
Inputs may be any that keep to these rules, and one draw needn't show every extreme that they name: tiles[b, k] is a tile id in block b's row group; the column index holding tile t is t // 512. Among the 32 entries of one device's blocks, at most 8 (repeats counted) name tiles held by one column index.
All inputs are finite; a program needn't handle non-finite values.
Results may differ from a plain program's by a relative error of at most 0.000071.
Values sent between devices are 32-bit elements; how exact they have to be, the bound alone decides.
A program may use at most 128 MiB of HBM per device.

v0:
```python
import jax
import jax.numpy as jnp
from jax import lax
from jax.sharding import PartitionSpec as P

NY = 2048
TY = 8
K = 4
CAP = 8


smoothing = 1.0


def tile_slots(requests, tile_count, columns):
    holder = requests // tile_count
    within = requests % tile_count
    hits = (holder[:, None] == jnp.arange(columns, dtype=jnp.int32)[None, :]).astype(jnp.int32)
    before = jnp.cumsum(hits, axis=0) - hits
    place = jnp.sum(before * hits, axis=1)
    return (holder, within, place)


def local(velocity, z_inverse, tiles, amplitude, lateral, vertical, wall_velocity, surface):
    width_x = velocity.shape[1]
    rows_y = velocity.shape[2]
    depth = velocity.shape[3]
    columns = lax.axis_size("col")
    per_row = rows_y // TY
    tile_count = width_x * per_row
    blocks = tiles.shape[0]
    requests = tiles.reshape(-1)
    request_count = requests.shape[0]
    holder, within, place = tile_slots(requests, tile_count, columns)
    target_slot = holder * CAP + place
    wanted = (
        jnp.zeros((columns * CAP,), jnp.int32).at[target_slot].set(within).reshape(columns, CAP)
    )
    served = lax.all_to_all(wanted, "col", split_axis=0, concat_axis=0, tiled=True)
    store = (
        velocity.reshape(3, width_x, per_row, TY, depth)
        .transpose(1, 2, 0, 3, 4)
        .reshape(tile_count, 3, TY, depth)
    )
    served_flat = served.reshape(-1)
    outgoing_tiles = store[served_flat].reshape(columns, CAP, 3, TY, depth)
    fetched = lax.all_to_all(
        outgoing_tiles, "col", split_axis=0, concat_axis=0, tiled=True
    ).reshape(columns * CAP, 3, TY, depth)
    mine = fetched[target_slot].reshape(blocks, K, 3, TY, depth)
    inner = jnp.einsum("bkcyz,bzi->bkcyi", mine, vertical, precision=lax.Precision.HIGHEST)
    weight = amplitude[:, :, None, :] * lateral[:, None, :, :]
    sampled = jnp.sum(weight[:, :, None] * inner, axis=(1, 3))
    marker_force = wall_velocity - sampled
    share = weight[:, :, None] * (surface[:, None, :] * marker_force)[:, None, :, None, :]
    spread = jnp.einsum("bkcyi,bzi->bkcyz", share, vertical, precision=lax.Precision.HIGHEST)
    spread = spread.reshape(request_count, 3, TY, depth)
    outgoing = jnp.zeros((columns * CAP, 3, TY, depth), jnp.float32).at[target_slot].set(spread)
    incoming = lax.all_to_all(
        outgoing.reshape(columns, CAP, 3, TY, depth), "col", split_axis=0, concat_axis=0, tiled=True
    )
    forced_store = store.at[served_flat].add(incoming.reshape(columns * CAP, 3, TY, depth))
    forced = (
        forced_store.reshape(width_x, per_row, 3, TY, depth)
        .transpose(2, 0, 1, 3, 4)
        .reshape(3, width_x, rows_y, depth)
    )
    depthwise = jnp.einsum(
        "cxyz,zw->xcwy",
        lax.all_to_all(forced, "row", split_axis=1, concat_axis=3, tiled=True),
        z_inverse,
        precision=lax.Precision.HIGHEST,
    )
    places = jnp.arange(NY, dtype=jnp.int32)
    wavenumber = jnp.arange(NY // 2, dtype=jnp.int32)
    phase = (places[:, None] * wavenumber[None, :] % NY).astype(jnp.float32) * (2.0 * jnp.pi / NY)
    wave = wavenumber.astype(jnp.float32)
    damping = (
        1.0 / (1.0 + 4.0 * smoothing * jnp.sin(jnp.pi * wave / NY) ** 2) / jnp.sqrt(jnp.float32(NY))
    )
    table = jnp.stack(
        [jnp.cos(phase) * damping[None, :], -jnp.sin(phase) * damping[None, :]], axis=1
    )
    spectrum = jnp.einsum(
        "xczy,ypk->pcxzk",
        lax.all_to_all(depthwise, "col", split_axis=2, concat_axis=3, tiled=True),
        table,
        precision=lax.Precision.HIGHEST,
    )
    return (spectrum, marker_force)


def solution(mesh):
    in_specs = (
        P(None, None, "col", "row"),
        P(),
        P(("row", "col"), None),
        P(("row", "col"), None, None),
        P(("row", "col"), None, None),
        P(("row", "col"), None, None),
        P(("row", "col"), None, None),
        P(("row", "col"), None),
    )
    out_specs = (P(None, None, "row", "col", None), P(("row", "col"), None, None))
    return jax.shard_map(local, mesh=mesh, in_specs=in_specs, out_specs=out_specs, check_vma=False)
```

profile of v0, /device:TPU:1, one launch (start us, length us, event | category | flops | bytes accessed | tf_op | source)
XLA Modules:
  0.0 395.4 jit_solution(15614283783323233217)
XLA Ops:
  0.6 0.0 copy-start
  0.6 0.8 copy.25
  1.5 0.1 reshape.303
  1.6 0.1 reshape.302
  1.7 0.1 fusion.22
  1.7 0.1 reduce_window_sum.11
  1.8 0.2 select_reduce_fusion
  2.0 0.7 scatter_custom_fusion
  2.7 0.7 all_to_all.38
  3.4 8.6 %all-to-all-start = ((s32[16,1,8]{2,1,0:T(1,128)}), s32[16,1,8]{2,1,0:T(1,128)S(1)}, u32[]{:S(2)}, u32[]{:S(2)}) async-start(s32[16,1,8]{2,1,0:T(1,128)} %bitcast.7), calls=%async_computation | async-start | bytes 16384 | tf_op jit(solution)/shard_map/all_to_all | solution.py:39
  12.0 6.1 %copy.24 = f32[3,32,16,8,128]{4,3,0,2,1:T(8,128)} copy(f32[3,32,16,8,128]{4,3,2,1,0:T(8,128)} %bitcast.72) | data formatting | bytes 12582912 | tf_op jit(solution)/shard_map/reshape | solution.py:41
  18.1 0.0 copy-start.2
  18.1 0.0 copy-start.3
  18.1 0.0 copy-start.4
  18.1 0.0 copy-start.5
  18.1 0.3 all-to-all-done
  18.3 0.5 broadcast.319
  18.8 0.7 reduce.3
  19.5 0.1 reshape.304
  19.6 4.6 %gather_fusion = f32[128,3,8,128]{3,2,1,0:T(8,128)} fusion(f32[512,3,8,128]{3,2,1,0:T(8,128)} %bitcast.65, s32[1024]{0:T(1024)S(1)} %pad_clamp_fusion.1), kind=kCustom, calls=%fused_computation | custom fusion | bytes 3146240 | tf_op jit(solution)/shard_map/gather | solution.py:46
  24.2 6.4 %all-to-all-start.1 = ((f32[16,8,3,8,128]{4,3,2,1,0:T(8,128)}), f32[16,8,3,8,128]{4,3,2,1,0:T(8,128)S(1)}, u32[]{:S(2)}, u32[]{:S(2)}) async-start(f32[16,8,3,8,128]{4,3,2,1,0:T(8,128)} %bitcast.10), calls=%async_computation.1 | async-start | bytes 3145728 | tf_op jit(solution)/shard_map/all_to_all | solution.py:47
  30.6 0.0 copy-done.2
  30.7 0.0 copy-done.3
  30.7 21.1 %all-to-all-done.1 = f32[16,8,3,8,128]{4,3,2,1,0:T(8,128)S(1)} async-done(((f32[16,8,3,8,128]{4,3,2,1,0:T(8,128)}), f32[16,8,3,8,128]{4,3,2,1,0:T(8,128)S(1)}, u32[]{:S(2)}, u32[]{:S(2)}) %all-to-all-start.1) | async-done | bytes 1572896 | tf_op jit(solution)/shard_map/all_to_all | solution.py:47
  51.8 0.6 gather_fusion.1
  52.4 0.0 copy-done
  52.4 0.9 fusion.15
  53.3 0.0 copy-done.4
  53.3 0.0 copy-done.5
  53.3 1.2 fusion.16
  54.6 0.1 broadcast_in_dim.2
  54.7 1.6 scatter_fusion
  56.2 27.8 %all_to_all.55 = f32[16,8,3,8,128]{4,3,2,1,0:T(8,128)} all-to-all(f32[16,8,3,8,128]{4,3,2,1,0:T(8,128)S(1)} %bitcast.71), channel_id=1, replica_groups=mesh['row'=8,'col'=16] {'col'}, dimensions={0} | all-to-all | bytes 3145728 | tf_op jit(solution)/shard_map/all_to_all | solution.py:59
  84.0 18.2 %scatter_fusion.1 = f32[512,3,8,128]{3,2,1,0:T(8,128)} fusion(f32[512,3,8,128]{3,2,1,0:T(8,128)} %bitcast.66, s32[128]{0:T(128)S(1)} %fusion.24, f32[128,3,8,128]{3,2,1,0:T(8,128)} %bitcast.73), kind=kCustom, calls=%fused_computation.4 | custom fusion | flops 393216 | bytes 4719104 | tf_op jit(solution)/shard_map/scatter-add | solution.py:62
  102.2 3.5 copy.44
  105.7 76.5 %all_to_all.56 = f32[3,32,128,128]{3,2,0,1:T(8,128)S(1)} all-to-all(f32[3,32,128,128]{3,2,0,1:T(8,128)S(1)} %bitcast.68), channel_id=1, replica_groups=mesh['row'=8,'col'=16] {'row'}, dimensions={1} | all-to-all | bytes 12582912 | tf_op jit(solution)/shard_map/all_to_all | solution.py:70
  182.2 7.1 %copy.31 = f32[3,4,128,8,128]{4,3,2,1,0:T(8,128)} copy(f32[3,4,128,8,128]{4,2,0,1,3:T(8,128)S(1)} %bitcast.69) | data formatting | bytes 12582912 | tf_op jit(solution)/shard_map/all_to_all | solution.py:70
  189.3 7.1 %all_to_all.45 = f32[3,4,128,1024]{3,2,1,0:T(8,128)} reshape(f32[3,4,128,8,128]{4,3,2,1,0:T(8,128)} %copy.31) | data formatting | bytes 12582912 | tf_op jit(solution)/shard_map/all_to_all | solution.py:70
  196.4 24.8 %fusion.11 = f32[4,3,1024,128]{2,3,0,1:T(8,128)} fusion(f32[3,4,128,1024]{3,2,1,0:T(8,128)} %all_to_all.45, f32[1024,1024]{1,0:T(8,128)} %param.9), kind=kOutput, calls=%fused_computation.23 | convolution fusion | flops 19327352832 | bytes 16777216 | tf_op jit(solution)/shard_map/cxyz,zw->xcwy/dot_general | solution.py:68
  221.2 7.6 %copy.32 = f32[4,3,1024,128]{3,0,1,2:T(4,128)} copy(f32[4,3,1024,128]{2,3,0,1:T(8,128)} %fusion.11) | data formatting | bytes 12582912 | tf_op jit(solution)/shard_map/cxyz,zw->xcwy/transpose | solution.py:68
  228.8 4.8 %all-to-all-start.4 = ((f32[4,3,1024,128]{3,0,1,2:T(4,128)}), f32[4,3,1024,128]{3,0,1,2:T(4,128)}, u32[]{:S(2)}, u32[]{:S(2)}) async-start(f32[4,3,1024,128]{3,0,1,2:T(4,128)} %copy.32), calls=%async_computation.4 | async-start | bytes 12582912 | tf_op jit(solution)/shard_map/all_to_all | solution.py:86
  233.7 35.2 %cosine_multiply_fusion = (f32[2048,1,1024]{2,0,1:T(8,128)}, f32[2048,1,1024]{2,0,1:T(8,128)}) fusion(f32[1024]{0:T(1024)S(1)} %divide_multiply_fusion), kind=kLoop, calls=%fused_computation.16 | loop fusion | flops 35651584 | bytes 16781312 | tf_op jit(solution)/shard_map/mul | solution.py:82
  268.9 0.6 copy.36
  269.5 56.2 %all-to-all-done.4 = f32[4,3,1024,128]{3,0,1,2:T(4,128)} async-done(((f32[4,3,1024,128]{3,0,1,2:T(4,128)}), f32[4,3,1024,128]{3,0,1,2:T(4,128)}, u32[]{:S(2)}, u32[]{:S(2)}) %all-to-all-start.4) | async-done | bytes 6291488 | tf_op jit(solution)/shard_map/all_to_all | solution.py:86
  325.7 3.3 copy.33
  329.0 7.1 %copy.34 = f32[4,3,64,16,128]{4,3,2,1,0:T(8,128)} copy(f32[4,3,64,16,128]{4,2,3,1,0:T(8,128)S(1)} %bitcast.70) | data formatting | bytes 12582912 | tf_op jit(solution)/shard_map/all_to_all | solution.py:86
  336.1 7.1 %reshape.356 = f32[4,3,64,2048,1]{3,2,1,0,4:T(8,128)} reshape(f32[4,3,64,16,128]{4,3,2,1,0:T(8,128)} %copy.34) | data formatting | bytes 12582912 | tf_op jit(solution)/shard_map/all_to_all | solution.py:86
  343.2 0.0 copy-start.1
  343.2 48.9 %fusion.14 = f32[2,3,4,64,1024]{4,3,1,2,0:T(8,128)S(1)} fusion(f32[4,3,64,2048,1]{3,2,1,0,4:T(8,128)} %reshape.356, f32[2048,1,1024]{2,0,1:T(8,128)} %get-tuple-element.11, f32[2048,1,1024]{2,0,1:T(8,128)} %get-tuple-element.10), kind=kOutput, calls=%fused_computation.24 | convolution fusion | flops 38658899968 | bytes 29360128 | tf_op jit(solution)/shard_map/xczy,ypk->pcxzk/dot_general | solution.py:84
  392.1 3.3 copy.35
  395.4 0.0 copy-done.1
  (8 shorter events, 0.1 us)
Async XLA Ops:
  0.6 51.8 %copy-start = (f32[8,128,256]{2,1,0:T(8,128)S(1)}, f32[8,128,256]{2,1,0:T(8,128)}, u32[]{:S(2)}) copy-start(f32[8,128,256]{2,1,0:T(8,128)} %param.13) | copy-start | bytes 3145732
  3.4 15.0 %all-to-all-start = ((s32[16,1,8]{2,1,0:T(1,128)}), s32[16,1,8]{2,1,0:T(1,128)S(1)}, u32[]{:S(2)}, u32[]{:S(2)}) async-start(s32[16,1,8]{2,1,0:T(1,128)} %bitcast.7), calls=%async_computation | async-start | bytes 16384 | tf_op jit(solution)/shard_map/all_to_all | solution.py:39
  18.1 12.6 %copy-start.2 = (f32[8,8,256]{2,1,0:T(8,128)S(1)}, f32[8,8,256]{2,1,0:T(8,128)}, u32[]{:S(2)}) copy-start(f32[8,8,256]{2,1,0:T(8,128)} %param.12) | copy-start | bytes 196612
  18.1 12.6 %copy-start.3 = (f32[8,4,256]{2,1,0:T(4,128)S(1)}, f32[8,4,256]{2,1,0:T(4,128)}, u32[]{:S(2)}) copy-start(f32[8,4,256]{2,1,0:T(4,128)} %param.11) | copy-start | bytes 98308
  18.1 35.2 %copy-start.4 = (f32[8,3,256]{2,0,1:T(8,128)S(1)}, f32[8,3,256]{2,0,1:T(8,128)}, u32[]{:S(2)}) copy-start(f32[8,3,256]{2,0,1:T(8,128)} %param.14) | copy-start | bytes 73732
  18.1 35.2 %copy-start.5 = (f32[8,256]{1,0:T(8,128)S(1)}, f32[8,256]{1,0:T(8,128)}, u32[]{:S(2)}) copy-start(f32[8,256]{1,0:T(8,128)} %param.15) | copy-start | bytes 24580
  24.2 27.6 %all-to-all-start.1 = ((f32[16,8,3,8,128]{4,3,2,1,0:T(8,128)}), f32[16,8,3,8,128]{4,3,2,1,0:T(8,128)S(1)}, u32[]{:S(2)}, u32[]{:S(2)}) async-start(f32[16,8,3,8,128]{4,3,2,1,0:T(8,128)} %bitcast.10), calls=%async_computation.1 | async-start | bytes 3145728 | tf_op jit(solution)/shard_map/all_to_all | solution.py:47
  228.8 96.9 %all-to-all-start.4 = ((f32[4,3,1024,128]{3,0,1,2:T(4,128)}), f32[4,3,1024,128]{3,0,1,2:T(4,128)}, u32[]{:S(2)}, u32[]{:S(2)}) async-start(f32[4,3,1024,128]{3,0,1,2:T(4,128)} %copy.32), calls=%async_computation.4 | async-start | bytes 12582912 | tf_op jit(solution)/shard_map/all_to_all | solution.py:86
  343.2 52.2 %copy-start.1 = (f32[8,128,256]{2,1,0:T(8,128)S(1)}, f32[8,128,256]{2,1,0:T(8,128)}, u32[]{:S(2)}) copy-start(f32[8,128,256]{2,1,0:T(8,128)} %param.13) | copy-start | bytes 3145732
where the time goes:
time: 397 us; the launch traced here: 395 us
  blocking collectives  104 us (26%)
  waiting for transfers between devices  77.6 us (20%)
  matrix products  75.8 us (19%)
  local copies, waits for them, and re-layouts  62.5 us (16%)
  other arithmetic  54.5 us (14%)
  starting transfers between devices  19.8 us (5%)
    all_to_all x1, blocking collectives, local(): lax.all_to_all(forced, 'row', split_axis=1, concat_axis=3, tiled=True)  76.5 us
    all_to_all x1, waiting for transfers between devices, local(): lax.all_to_all(depthwise, 'col', split_axis=2, concat_axis=3, tiled=True)  56.2 us
    dot_general x1, matrix products, local(): jnp.einsum('xczy,ypk->pcxzk', lax.all_to_all(depthwise, 'col', split_axis...  48.9 us
    mul x1, other arithmetic, local(): jnp.cos(phase) * damping[None, :]  35.2 us
    all_to_all x1, blocking collectives, local(): lax.all_to_all(outgoing.reshape(columns, CAP, 3, TY, depth), 'col', split...  27.8 us
    dot_general x1, matrix products, local(): jnp.einsum('cxyz,zw->xcwy', lax.all_to_all(forced, 'row', split_axis=1, c...  24.8 us
    all_to_all x1, waiting for transfers between devices, local(): lax.all_to_all(outgoing_tiles, 'col', split_axis=0, concat_axis=0, tiled=...  21.1 us
    scatter-add x1, other arithmetic, local(): store.at[served_flat].add(incoming.reshape(columns * CAP, 3, TY, depth))  18.2 us
  transfers between devices with their start and end apart: 3, of which 3 were waited for; matrix products, arithmetic and copies ran while one was open for 11% of the time, Pallas kernels for 0%

commit v1 on v0

v1 whole, which is shorter than its diff:
```python
import functools
import numpy as np
import jax
import jax.numpy as jnp
from jax import lax
from jax.experimental import pallas as pl
from jax.experimental.pallas import tpu as pltpu
from jax.sharding import PartitionSpec as P

NY = 2048
TY = 8
K = 4
CAP = 8
TILES = 512
ROWS = 8
COLS = 16
SLOTS = COLS * CAP
REQ = 32
CHUNKS = 6

smoothing = 1.0

MESH = pl.DeviceIdType.MESH
F32 = jnp.float32
BF16 = jnp.bfloat16


def split(x):
    hi = x.astype(BF16)
    lo = (x - hi.astype(F32)).astype(BF16)
    return hi, lo


def dot(a, b, dims=((1,), (0,))):
    return lax.dot_general(a, b, (dims, ((), ())), preferred_element_type=F32)


def tables():
    k1 = np.arange(256)
    y2 = np.arange(256)
    phase = 2.0 * np.pi * ((k1[:, None] * y2[None, :]) % 256) / 256.0
    table = np.concatenate([np.cos(phase), -np.sin(phase)], axis=0).astype(np.float32)
    y1 = np.arange(8)
    turn = 2.0 * np.pi * (k1[:, None] * y1[None, :]) / NY
    twiddle = np.zeros((256, 128), np.float32)
    twiddle[:, 0:8] = np.cos(turn)
    twiddle[:, 8:16] = np.sin(turn)
    wave = np.arange(NY // 2, dtype=np.float64)
    damping = 1.0 / (1.0 + 4.0 * smoothing * np.sin(np.pi * wave / NY) ** 2) / np.sqrt(NY)
    return table, twiddle, damping.astype(np.float32)[None, :]


def kernel(
    vel, zinv, wanted, take_at, give_at, amp, lat, vert, wall, surf, table, tw_in, damp,
    out, force_out,
    v, zf, zh, zl, vth, vtl, weight, tab_h, tab_l, tw, ids, pick, put, take, give,
    fo, fr, spread, ro, ri, g, xh, s, h, u, xk, ob,
    load_sem, id_send, id_recv, f_send, f_recv, b_send, b_recv,
    r_send, r_recv, c_send, c_recv, o_sem,
):
    row = lax.axis_index("row")
    col = lax.axis_index("col")
    x = row // 2
    core = lax.rem(row, 2)
    z = col // 4
    y = lax.rem(col, 4)

    def row_peer(d):
        return lax.rem(x + d // 2, 4) * 2 + lax.rem(core + lax.rem(d, 2), 2)

    def col_peer(d):
        return lax.rem(z + d // 4, 4) * 4 + lax.rem(y + lax.rem(d, 4), 4)

    def rows(i, n):
        return pl.ds(pl.multiple_of(i * n, n), n)

    vel_copy = pltpu.make_async_copy(vel, v, load_sem.at[0])
    vel_copy.start()
    zinv_copy = pltpu.make_async_copy(zinv, zf, load_sem.at[1])
    zinv_copy.start()

    barrier = pltpu.get_barrier_semaphore()

    def greet_row(d, _):
        pl.semaphore_signal(barrier, 1, device_id={"row": row_peer(d)}, device_id_type=MESH)
        return 0

    def greet_col(d, _):
        pl.semaphore_signal(barrier, 1, device_id={"col": col_peer(d)}, device_id_type=MESH)
        return 0

    lax.fori_loop(1, COLS, greet_col, 0)
    lax.fori_loop(1, ROWS, greet_row, 0)

    def prepare(b, _):
        hi, lo = split(vert[b])
        vth[b] = hi
        vtl[b] = lo
        for k in range(K):
            weight[b, k * TY : (k + 1) * TY, :] = amp[b, k : k + 1, :] * lat[b]
        return 0

    lax.fori_loop(0, 8, prepare, 0)

    pl.semaphore_wait(barrier, ROWS + COLS - 2)

    def id_copy(peer):
        return pltpu.make_async_remote_copy(
            wanted.at[peer], ids.at[col], id_send.at[peer], id_recv.at[col],
            device_id={"col": peer}, device_id_type=MESH,
        )

    def id_wait(peer):
        pltpu.make_async_remote_copy(
            wanted.at[peer], ids.at[peer], id_send.at[peer], id_recv.at[peer],
            device_id={"col": peer}, device_id_type=MESH,
        ).wait_recv()

    def f_copy(c, peer):
        return pltpu.make_async_remote_copy(
            fo.at[c, rows(peer, 64)], fr.at[c, rows(col, 64)], f_send.at[c, peer], f_recv.at[c, col],
            device_id={"col": peer}, device_id_type=MESH,
        )

    def f_wait(c, peer):
        pltpu.make_async_remote_copy(
            fo.at[c, rows(peer, 64)], fr.at[c, rows(peer, 64)], f_send.at[c, peer], f_recv.at[c, peer],
            device_id={"col": peer}, device_id_type=MESH,
        ).wait_recv()

    def b_copy(c, peer):
        return pltpu.make_async_remote_copy(
            ro.at[c, rows(peer, 64)], ri.at[c, rows(col, 64)], b_send.at[c, peer], b_recv.at[c, col],
            device_id={"col": peer}, device_id_type=MESH,
        )

    def b_wait(c, peer):
        pltpu.make_async_remote_copy(
            ro.at[c, rows(peer, 64)], ri.at[c, rows(peer, 64)], b_send.at[c, peer], b_recv.at[c, peer],
            device_id={"col": peer}, device_id_type=MESH,
        ).wait_recv()

    def r_rows(n, peer):
        return pl.ds(pl.multiple_of((peer * 4 + 2 * lax.rem(n, 2)) * 128, 256), 256)

    def r_copy(n, peer):
        return pltpu.make_async_remote_copy(
            v.at[n // 2, r_rows(n, peer)], g.at[n, row], r_send.at[n, peer], r_recv.at[n, row],
            device_id={"row": peer}, device_id_type=MESH,
        )

    def r_wait(n, peer):
        pltpu.make_async_remote_copy(
            v.at[n // 2, r_rows(n, peer)], g.at[n, peer], r_send.at[n, peer], r_recv.at[n, peer],
            device_id={"row": peer}, device_id_type=MESH,
        ).wait_recv()

    def c_copy(n, peer):
        return pltpu.make_async_remote_copy(
            s.at[n, rows(peer, 128)], h.at[n, rows(col, 128)], c_send.at[n, peer], c_recv.at[n, col],
            device_id={"col": peer}, device_id_type=MESH,
        )

    def c_wait(n, peer):
        pltpu.make_async_remote_copy(
            s.at[n, rows(peer, 128)], h.at[n, rows(peer, 128)], c_send.at[n, peer], c_recv.at[n, peer],
            device_id={"col": peer}, device_id_type=MESH,
        ).wait_recv()

    def each_col(do):
        def step(d, _):
            do(col_peer(d))
            return 0

        lax.fori_loop(1, COLS, step, 0)

    def each_row(do):
        def step(d, _):
            do(row_peer(d))
            return 0

        lax.fori_loop(1, ROWS, step, 0)

    each_col(lambda p: id_copy(p).start())
    ids[col] = wanted[col]
    vel_copy.wait()
    each_col(id_wait)
    id_all = ids[...].reshape(SLOTS, 128)
    lane = lax.broadcasted_iota(jnp.int32, (128, 128), 1)
    for j in range(4):
        hit = jnp.where(id_all == lane + 128 * j, 1.0, 0.0).astype(F32)
        at = slice(j * 128, (j + 1) * 128)
        pick[:, at] = hit.astype(BF16)
        hit = hit.T.astype(BF16)
        put[at, 0:128] = hit
        put[at, 128:256] = hit

    def pair(ref, c, q, n):
        a = ref[c, pl.ds(2 * q, n, stride=TY), :]
        b = ref[c, pl.ds(2 * q + 1, n, stride=TY), :]
        return split(jnp.concatenate([a, b], axis=1))

    def gather(c):
        for q in range(4):
            hi, lo = pair(v, c, q, TILES)
            got = dot(pick[...], hi) + dot(pick[...], lo)
            for e in range(2):
                fo[c, pl.ds(2 * q + e, SLOTS, stride=TY), :] = got[:, e * 128 : (e + 1) * 128]
        each_col(lambda p: f_copy(c, p).start())
        fr[c, rows(col, 64), :] = fo[c, rows(col, 64), :]

    gather(0)
    gather(1)

    def select(at_ref, to, count, width):
        def block(i, _):
            at = rows(i, 128)
            for j in range(width // 128):
                hit = jnp.where(at_ref[at, :] == lane + 128 * j, 1.0, 0.0)
                to[at, j * 128 : (j + 1) * 128] = hit.astype(BF16)
            return 0

        lax.fori_loop(0, count // 128, block, 0)

    select(take_at, take, REQ * TY, SLOTS * TY)
    select(give_at, give, SLOTS * TY, REQ * TY)

    hi, lo = split(table[...])
    tab_h[...] = hi
    tab_l[...] = lo
    for i in range(16):
        tw[i] = jnp.broadcast_to(tw_in[:, i : i + 1], (256, 128))

    zinv_copy.wait()

    def cut(i, _):
        at = rows(i, 128)
        for j in range(4):
            hi, lo = split(zf[at, j * 256 : (j + 1) * 256])
            zh[j, at, :] = hi
            zl[j, at, :] = lo
        return 0

    lax.fori_loop(0, 8, cut, 0)

    def markers(c):
        each_col(lambda p: f_wait(c, p))
        f_hi, f_lo = split(fr[c])
        mine = dot(take[...], f_hi) + dot(take[...], f_lo)
        for b in range(8):
            at = slice(b * K * TY, (b + 1) * K * TY)
            p_hi, p_lo = split(mine[at, :])
            inner = dot(p_hi, vth[b]) + (dot(p_lo, vth[b]) + dot(p_hi, vtl[b]))
            w = weight[b]
            sampled = jnp.sum(w * inner, axis=0, keepdims=True)
            force = wall[c, b : b + 1, :] - sampled
            force_out[c, b : b + 1, :] = force
            s_hi, s_lo = split(w * (surf[b : b + 1, :] * force))
            last = ((1,), (1,))
            back = dot(s_hi, vth[b], last) + (dot(s_lo, vth[b], last) + dot(s_hi, vtl[b], last))
            spread[at, :] = back
        b_hi, b_lo = split(spread[...])
        ro[c] = dot(give[...], b_hi) + dot(give[...], b_lo)
        each_col(lambda p: b_copy(c, p).start())
        ri[c, rows(col, 64), :] = ro[c, rows(col, 64), :]

    def force_tiles(c):
        each_col(lambda p: b_wait(c, p))
        for q in range(4):
            hi, lo = pair(ri, c, q, SLOTS)
            delta = dot(put[...], jnp.concatenate([hi, lo], axis=0))
            for e in range(2):
                at = pl.ds(2 * q + e, TILES, stride=TY)
                v[c, at, :] = v[c, at, :] + delta[:, e * 128 : (e + 1) * 128]
        for e in range(2):
            n = 2 * c + e
            each_row(lambda p: r_copy(n, p).start())
            g[n, row] = v[c, r_rows(n, row), :]

    def first(c, _):
        @pl.when(c < 3)
        def _():
            markers(c)

        @pl.when(c == 0)
        def _():
            gather(2)

        @pl.when(c > 0)
        def _():
            force_tiles(c - 1)

        return 0

    lax.fori_loop(0, 4, first, 0)

    low = lane < 64

    def axial(n):
        each_row(lambda p: r_wait(n, p))
        for r in range(ROWS):
            hi, lo = split(g[n, r])
            xh[0:256, r * 128 : (r + 1) * 128] = hi
            xh[256:512, r * 128 : (r + 1) * 128] = lo

        def tile(j, _):
            acc = dot(xh[...], zh[j])
            acc = acc[0:256] + (acc[256:512] + dot(xh[0:256, :], zl[j]))
            for t in range(2):
                a0 = acc[0:128, t * 128 : (t + 1) * 128]
                a1 = acc[128:256, t * 128 : (t + 1) * 128]
                s[n, rows(4 * j + 2 * t, 128), :] = jnp.where(low, a0, pltpu.roll(a1, 64, 1))
                s[n, rows(4 * j + 2 * t + 1, 128), :] = jnp.where(low, pltpu.roll(a0, 64, 1), a1)
            return 0

        lax.fori_loop(0, 4, tile, 0)
        each_col(lambda p: c_copy(n, p).start())
        h[n, rows(col, 128), :] = s[n, rows(col, 128), :]

    def out_copy(n):
        return pltpu.make_async_copy(ob.at[n], out.at[:, n // 2, lax.rem(n, 2)], o_sem.at[n])

    half = np.float32(np.sqrt(0.5))

    def fourier(n):
        each_col(lambda p: c_wait(n, p))
        for q in range(4):
            a = h[n, pl.ds(2 * q, 256, stride=8), :]
            b = h[n, pl.ds(2 * q + 1, 256, stride=8), :]
            hi, lo = split(jnp.concatenate([a, b], axis=1))
            acc = dot(tab_h[...], hi) + (dot(tab_h[...], lo) + dot(tab_l[...], hi))
            u[2 * q] = acc[:, 0:128]
            u[2 * q + 1] = acc[:, 128:256]

        def combine(i, _):
            re = rows(i, 8)
            im = pl.ds(pl.multiple_of(256 + i * 8, 8), 8)
            a = []
            for m in range(8):
                ur, ui = u[m, re, :], u[m, im, :]
                if m > 0:
                    tc, ts = tw[m, re, :], tw[8 + m, re, :]
                    ur, ui = ur * tc + ui * ts, ui * tc - ur * ts
                a.append((ur, ui))

            def add(p, q):
                return (p[0] + q[0], p[1] + q[1])

            def sub(p, q):
                return (p[0] - q[0], p[1] - q[1])

            def turn(p):
                return (p[1], -p[0])

            def four(p, q, r, t):
                s0, d0, s1, d1 = add(p, r), sub(p, r), add(q, t), turn(sub(q, t))
                return add(s0, s1), add(d0, d1), sub(s0, s1), sub(d0, d1)

            e0, e1, e2, e3 = four(a[0], a[2], a[4], a[6])
            o0, o1, o2, o3 = four(a[1], a[3], a[5], a[7])
            o1 = ((o1[0] + o1[1]) * half, (o1[1] - o1[0]) * half)
            o3 = ((o3[1] - o3[0]) * half, (-o3[1] - o3[0]) * half)
            for k2, (e, o) in enumerate(((e0, o0), (e1, o1), (e2, turn(o2)), (e3, o3))):
                xr, xi = add(e, o)
                xk[0, k2, re, :] = xr
                xk[1, k2, re, :] = xi
            return 0

        lax.fori_loop(0, 32, combine, 0, unroll=2)
        for p in range(2):
            for k2 in range(4):
                at = slice(k2 * 256, (k2 + 1) * 256)
                ob[n, p, :, at] = xk[p, k2].T * damp[:, at]
        out_copy(n).start()

    def second(n, _):
        @pl.when(n < CHUNKS)
        def _():
            axial(n)

        @pl.when(n > 0)
        def _():
            fourier(n - 1)

        return 0

    lax.fori_loop(0, CHUNKS + 1, second, 0)

    each_col(lambda p: id_copy(p).wait_send())

    def drain3(c, _):
        each_col(lambda p: f_copy(c, p).wait_send())
        each_col(lambda p: b_copy(c, p).wait_send())
        return 0

    def drain6(n, _):
        each_row(lambda p: r_copy(n, p).wait_send())
        each_col(lambda p: c_copy(n, p).wait_send())
        out_copy(n).wait()
        return 0

    lax.fori_loop(0, 3, drain3, 0)
    lax.fori_loop(0, CHUNKS, drain6, 0)


def local(velocity, z_inverse, tiles, amplitude, lateral, vertical, wall_velocity, surface):
    wants = tiles.reshape(-1)
    holder = wants // TILES
    within = wants % TILES
    order = jnp.arange(REQ, dtype=jnp.int32)
    before = (holder[:, None] == holder[None, :]) & (order[None, :] < order[:, None])
    slot_of = holder * CAP + jnp.sum(before.astype(jnp.int32), axis=1)
    match = jnp.arange(SLOTS, dtype=jnp.int32)[:, None] == slot_of[None, :]
    wanted = jnp.sum(jnp.where(match, within[None, :], 0), axis=1)
    source = jnp.sum(jnp.where(match, order[None, :] - REQ, 0), axis=1) + REQ
    wanted = jnp.broadcast_to(wanted[:, None], (SLOTS, 128)).reshape(COLS, CAP, 128)
    line = jnp.arange(TY, dtype=jnp.int32)

    def spread_out(index):
        cells = index[:, None, None] * TY + line[None, :, None]
        return jnp.broadcast_to(cells, (index.shape[0], TY, 128)).reshape(-1, 128)

    table, twiddle, damping = tables()
    any_ = pl.BlockSpec(memory_space=pl.ANY)
    vmem = pl.BlockSpec(memory_space=pltpu.VMEM)
    dma = pltpu.SemaphoreType.DMA
    spectrum, force = pl.pallas_call(
        kernel,
        out_shape=(
            jax.ShapeDtypeStruct((2, 3, 2, 128, 1024), F32),
            jax.ShapeDtypeStruct((3, 8, 256), F32),
        ),
        in_specs=[any_, any_] + [vmem] * 11,
        out_specs=(any_, vmem),
        scratch_shapes=[
            pltpu.VMEM((3, 4096, 128), F32),
            pltpu.VMEM((1024, 1024), F32),
            pltpu.VMEM((4, 1024, 256), BF16),
            pltpu.VMEM((4, 1024, 256), BF16),
            pltpu.VMEM((8, 128, 256), BF16),
            pltpu.VMEM((8, 128, 256), BF16),
            pltpu.VMEM((8, 32, 256), F32),
            pltpu.VMEM((512, 256), BF16),
            pltpu.VMEM((512, 256), BF16),
            pltpu.VMEM((16, 256, 128), F32),
            pltpu.VMEM((COLS, CAP, 128), jnp.int32),
            pltpu.VMEM((SLOTS, TILES), BF16),
            pltpu.VMEM((TILES, 2 * SLOTS), BF16),
            pltpu.VMEM((REQ * TY, SLOTS * TY), BF16),
            pltpu.VMEM((SLOTS * TY, REQ * TY), BF16),
            pltpu.VMEM((3, SLOTS * TY, 128), F32),
            pltpu.VMEM((3, SLOTS * TY, 128), F32),
            pltpu.VMEM((REQ * TY, 128), F32),
            pltpu.VMEM((3, SLOTS * TY, 128), F32),
            pltpu.VMEM((3, SLOTS * TY, 128), F32),
            pltpu.VMEM((CHUNKS, ROWS, 256, 128), F32),
            pltpu.VMEM((512, 1024), BF16),
            pltpu.VMEM((CHUNKS, NY, 128), F32),
            pltpu.VMEM((CHUNKS, NY, 128), F32),
            pltpu.VMEM((8, 512, 128), F32),
            pltpu.VMEM((2, 4, 256, 128), F32),
            pltpu.VMEM((CHUNKS, 2, 128, 1024), F32),
            dma((2,)),
            dma((COLS,)), dma((COLS,)),
            dma((3, COLS)), dma((3, COLS)),
            dma((3, COLS)), dma((3, COLS)),
            dma((CHUNKS, ROWS)), dma((CHUNKS, ROWS)),
            dma((CHUNKS, COLS)), dma((CHUNKS, COLS)),
            dma((CHUNKS,)),
        ],
        compiler_params=pltpu.CompilerParams(
            collective_id=0, has_side_effects=True, vmem_limit_bytes=60 * 1024 * 1024
        ),
        name="slab",
    )(
        velocity.reshape(3, 4096, 128), z_inverse, wanted, spread_out(slot_of), spread_out(source),
        amplitude, lateral, vertical, wall_velocity.transpose(1, 0, 2), surface,
        jnp.asarray(table), jnp.asarray(twiddle), jnp.asarray(damping),
    )
    return (spectrum.reshape(2, 3, 4, 64, 1024), force.transpose(1, 0, 2))


def solution(mesh):
    in_specs = (
        P(None, None, "col", "row"),
        P(),
        P(("row", "col"), None),
        P(("row", "col"), None, None),
        P(("row", "col"), None, None),
        P(("row", "col"), None, None),
        P(("row", "col"), None, None),
        P(("row", "col"), None),
    )
    out_specs = (P(None, None, "row", "col", None), P(("row", "col"), None, None))
    return jax.shard_map(local, mesh=mesh, in_specs=in_specs, out_specs=out_specs, check_vma=False)
```

time: 397 us -> 158 us (0.40)
  Pallas kernels: 0 us -> 146 us
  blocking collectives: 104 us -> 0 us
  waiting for transfers between devices: 77.6 us -> 0 us
  matrix products: 75.8 us -> 0 us
  other arithmetic: 54.5 us -> 0.45 us
  local copies, waits for them, and re-layouts: 62.5 us -> 10.8 us
  starting transfers between devices: 19.8 us -> 0 us
    pallas_call x0 -> x1, Pallas kernels: none -> 146 us  [local(): pl.pallas_call(kernel, out_shape=(jax.ShapeDtypeStruct((2, 3, 2, 128, 102...]
    all_to_all x2 -> x0, blocking collectives: 104 us -> none  [the longest x1 76.5 us: local(): lax.all_to_all(forced, 'row', split_axis=1, concat_axis=3, tiled=True)]
    all_to_all x3 -> x0, waiting for transfers between devices: 77.6 us -> none  [the longest x1 56.2 us: local(): lax.all_to_all(depthwise, 'col', split_axis=2, concat_axis=3, tiled=True)]
    dot_general x4 -> x0, matrix products: 75.8 us -> none  [the longest x1 48.9 us: local(): jnp.einsum('xczy,ypk->pcxzk', lax.all_to_all(depthwise, 'col', split_axis...]
    mul x3 -> x2, other arithmetic: 35.2 us -> 0.01 us  [spread_out(): cells = index[:, None, None] * TY + line[None, :, None]]
    all_to_all x7 -> x0, local copies, waits for them, and re-layouts: 32.8 us -> none  [the longest x3 17.5 us: local(): lax.all_to_all(depthwise, 'col', split_axis=2, concat_axis=3, tiled=True)]
    all_to_all x3 -> x0, starting transfers between devices: 19.8 us -> none  [the longest x1 8.59 us: local(): lax.all_to_all(wanted, 'col', split_axis=0, concat_axis=0, tiled=True)]
    scatter-add x1 -> x0, other arithmetic: 18.2 us -> none  [local(): store.at[served_flat].add(incoming.reshape(columns * CAP, 3, TY, depth))]
  transfers between devices with their start and end apart: 3 -> 0, of which waited for: 3 -> 0; matrix products, arithmetic and copies ran while one was open for 11% -> 0% of each run, Pallas kernels for 0% -> 0%
where the time goes in v1:
time: 158 us
  Pallas kernels  146 us (92%)
  local copies, waits for them, and re-layouts  10.8 us (7%)
    pallas_call x1, Pallas kernels, local(): pl.pallas_call(kernel, out_shape=(jax.ShapeDtypeStruct((2, 3, 2, 128, 102...  146 us
    unnamed x5, local copies, waits for them, and re-layouts  7.99 us

profile of v1, /device:TPU:1, one launch (start us, length us, event | category | flops | bytes accessed | tf_op | source)
XLA Modules:
  0.0 158.2 jit_solution(4973666337333277722)
XLA Ops:
  0.6 0.8 copy.15
  1.4 0.1 reshape.205
  1.5 0.2 convert_reduce_fusion
  1.7 0.1 select_reduce_fusion
  1.8 0.1 broadcast_in_dim.28
  1.9 0.1 iota_add_fusion.1
  1.9 0.1 add.100
  2.0 0.7 broadcast_in_dim.29.wanted
  2.7 0.1 iota_add_fusion
  2.8 0.1 add.106
  2.9 0.7 broadcast_in_dim.52.take_at
  3.7 1.0 broadcast_in_dim.54.give_at
  4.7 146.3 %slab.1 = (f32[2,3,2,128,1024]{4,3,2,1,0:T(8,128)}, f32[3,8,256]{2,1,0:T(8,128)}) custom-call(f32[3,4096,128]{2,1,0:T(8,128)} %bitcast.4, f32[1024,1024]{1,0:T(8,128)} %zinv.1, s32[16,8,128]{2,1,0:T(8,128)} %broadcast_in_dim.29.wanted, s32[256,128]{1,0:T(8,128)} %broadcast_in_dim.52.take_at, s32[1024,128]{1,0:T(8,128)} %broadcast_in_dim.54.give_at, ...), custom_call_target="tpu_custom_call" | custom-call | tf_op jit(solution)/shard_map/slab/pallas_call | solution.py:427
  151.0 0.0 copy-start
  151.0 6.6 %copy.18 = f32[2,3,4,64,1024]{4,3,2,1,0:T(8,128)} copy(f32[2,3,4,64,1024]{4,3,2,1,0:T(8,128)} %bitcast.5) | data formatting | bytes 12582912
  157.6 0.0 copy-done
  157.6 0.6 copy.19
  (3 shorter events, 0.0 us)
Async XLA Ops:
  151.0 6.6 %copy-start = (f32[3,8,256]{2,1,0:T(8,128)S(1)}, f32[3,8,256]{2,1,0:T(8,128)}, u32[]{:S(2)}) copy-start(f32[3,8,256]{2,1,0:T(8,128)} %get-tuple-element.5) | copy-start | bytes 73732

commit v2 on v1

--- a/solution.py
+++ b/solution.py
@@ -51,8 +51,9 @@
 
 
 def kernel(
-    vel, zinv, wanted, take_at, give_at, amp, lat, vert, wall, surf, table, tw_in, damp,
+    vel, zinv, tiles_in, amp_in, lat_in, vert_in, wall_in, surf_in, table_in, tw_hbm, damp_in,
     out, force_out,
+    tiles, amp, lat, vert, wall, surf, table, tw_in, damp, wanted,
     v, zf, zh, zl, vth, vtl, weight, tab_h, tab_l, tw, ids, pick, put, take, give,
     fo, fr, spread, ro, ri, g, xh, s, h, u, xk, ob,
     load_sem, id_send, id_recv, f_send, f_recv, b_send, b_recv,
@@ -74,11 +75,6 @@
     def rows(i, n):
         return pl.ds(pl.multiple_of(i * n, n), n)
 
-    vel_copy = pltpu.make_async_copy(vel, v, load_sem.at[0])
-    vel_copy.start()
-    zinv_copy = pltpu.make_async_copy(zinv, zf, load_sem.at[1])
-    zinv_copy.start()
-
     barrier = pltpu.get_barrier_semaphore()
 
     def greet_row(d, _):
@@ -92,6 +88,108 @@
     lax.fori_loop(1, COLS, greet_col, 0)
     lax.fori_loop(1, ROWS, greet_row, 0)
 
+    pairs = (
+        (tiles_in, tiles), (vert_in, vert), (amp_in, amp), (lat_in, lat), (vel, v), (zinv, zf),
+        (wall_in, wall), (surf_in, surf), (table_in, table), (tw_hbm, tw_in), (damp_in, damp),
+    )
+    loads = [pltpu.make_async_copy(a, b, load_sem.at[i]) for i, (a, b) in enumerate(pairs)]
+    for load in loads:
+        load.start()
+
+    loads[0].wait()
+    wants = [tiles[n // 8, n % 8] for n in range(REQ)]
+    holders = [lax.shift_right_logical(w, 9) for w in wants]
+    slots = []
+    for n in range(REQ):
+        rank = 0
+        for m in range(n):
+            rank = rank + (holders[m] == holders[n]).astype(jnp.int32)
+        slots.append(holders[n] * CAP + rank)
+    lane = lax.broadcasted_iota(jnp.int32, (128, 128), 1)
+    place = lax.broadcasted_iota(jnp.int32, (SLOTS, 128), 0)
+    named = jnp.zeros((SLOTS, 128), jnp.int32)
+    for n in range(REQ):
+        named = jnp.where(place == slots[n], wants[n] - holders[n] * TILES, named)
+    wanted[...] = named.reshape(COLS, CAP, 128)
+
+    pl.semaphore_wait(barrier, ROWS + COLS - 2)
+
+    east = col_peer(1)
+    north = row_peer(2)
+
+    def to_col(a, b, sems, peer):
+        return pltpu.make_async_remote_copy(
+            a, b, sems[0], sems[1], device_id={"col": peer}, device_id_type=MESH
+        )
+
+    def to_row(a, b, sems, peer):
+        return pltpu.make_async_remote_copy(
+            a, b, sems[0], sems[1], device_id={"row": peer}, device_id_type=MESH
+        )
+
+    id_sems = (id_send.at[0], id_recv.at[0])
+
+    def id_copy(peer):
+        return to_col(wanted.at[peer], ids.at[col], id_sems, peer)
+
+    def id_all_copies():
+        rest = pl.ds(0, COLS - 1)
+        return to_col(wanted.at[rest], ids.at[rest], id_sems, east)
+
+    many = pl.ds(0, (COLS - 1) * 64)
+
+    def f_copy(c, peer):
+        sems = (f_send.at[c], f_recv.at[c])
+        return to_col(fo.at[c, rows(peer, 64)], fr.at[c, rows(col, 64)], sems, peer)
+
+    def f_all(c):
+        return to_col(fo.at[c, many], fr.at[c, many], (f_send.at[c], f_recv.at[c]), east)
+
+    def b_copy(c, peer):
+        sems = (b_send.at[c], b_recv.at[c])
+        return to_col(ro.at[c, rows(peer, 64)], ri.at[c, rows(col, 64)], sems, peer)
+
+    def b_all(c):
+        return to_col(ro.at[c, many], ri.at[c, many], (b_send.at[c], b_recv.at[c]), east)
+
+    def r_rows(n, peer):
+        return pl.ds(pl.multiple_of((peer * 4 + 2 * lax.rem(n, 2)) * 128, 256), 256)
+
+    def r_copy(n, peer):
+        sems = (r_send.at[n], r_recv.at[n])
+        return to_row(v.at[n // 2, r_rows(n, peer)], g.at[n, rows(row, 256)], sems, peer)
+
+    def r_all(n):
+        most = pl.ds(0, (ROWS - 1) * 256)
+        return to_row(v.at[n // 2, most], g.at[n, most], (r_send.at[n], r_recv.at[n]), north)
+
+    def c_copy(n, peer):
+        sems = (c_send.at[n], c_recv.at[n])
+        return to_col(s.at[n, rows(peer, 128)], h.at[n, rows(col, 128)], sems, peer)
+
+    def c_all(n):
+        most = pl.ds(0, (COLS - 1) * 128)
+        return to_col(s.at[n, most], h.at[n, most], (c_send.at[n], c_recv.at[n]), east)
+
+    def each_col(do):
+        def step(d, _):
+            do(col_peer(d))
+            return 0
+
+        lax.fori_loop(1, COLS, step, 0)
+
+    def each_row(do):
+        def step(d, _):
+            do(row_peer(d))
+            return 0
+
+        lax.fori_loop(1, ROWS, step, 0)
+
+    each_col(lambda p: id_copy(p).start())
+    ids[col] = wanted[col]
+
+    for load in loads[1:4] + loads[8:10]:
+        load.wait()
     def prepare(b, _):
         hi, lo = split(vert[b])
         vth[b] = hi
@@ -102,91 +200,33 @@
 
     lax.fori_loop(0, 8, prepare, 0)
 
-    pl.semaphore_wait(barrier, ROWS + COLS - 2)
-
-    def id_copy(peer):
-        return pltpu.make_async_remote_copy(
-            wanted.at[peer], ids.at[col], id_send.at[peer], id_recv.at[col],
-            device_id={"col": peer}, device_id_type=MESH,
-        )
-
-    def id_wait(peer):
-        pltpu.make_async_remote_copy(
-            wanted.at[peer], ids.at[peer], id_send.at[peer], id_recv.at[peer],
-            device_id={"col": peer}, device_id_type=MESH,
-        ).wait_recv()
-
-    def f_copy(c, peer):
-        return pltpu.make_async_remote_copy(
-            fo.at[c, rows(peer, 64)], fr.at[c, rows(col, 64)], f_send.at[c, peer], f_recv.at[c, col],
-            device_id={"col": peer}, device_id_type=MESH,
-        )
-
-    def f_wait(c, peer):
-        pltpu.make_async_remote_copy(
-            fo.at[c, rows(peer, 64)], fr.at[c, rows(peer, 64)], f_send.at[c, peer], f_recv.at[c, peer],
-            device_id={"col": peer}, device_id_type=MESH,
-        ).wait_recv()
-
-    def b_copy(c, peer):
-        return pltpu.make_async_remote_copy(
-            ro.at[c, rows(peer, 64)], ri.at[c, rows(col, 64)], b_send.at[c, peer], b_recv.at[c, col],
-            device_id={"col": peer}, device_id_type=MESH,
-        )
-
-    def b_wait(c, peer):
-        pltpu.make_async_remote_copy(
-            ro.at[c, rows(peer, 64)], ri.at[c, rows(peer, 64)], b_send.at[c, peer], b_recv.at[c, peer],
-            device_id={"col": peer}, device_id_type=MESH,
-        ).wait_recv()
-
-    def r_rows(n, peer):
-        return pl.ds(pl.multiple_of((peer * 4 + 2 * lax.rem(n, 2)) * 128, 256), 256)
-
-    def r_copy(n, peer):
-        return pltpu.make_async_remote_copy(
-            v.at[n // 2, r_rows(n, peer)], g.at[n, row], r_send.at[n, peer], r_recv.at[n, row],
-            device_id={"row": peer}, device_id_type=MESH,
-        )
-
-    def r_wait(n, peer):
-        pltpu.make_async_remote_copy(
-            v.at[n // 2, r_rows(n, peer)], g.at[n, peer], r_send.at[n, peer], r_recv.at[n, peer],
-            device_id={"row": peer}, device_id_type=MESH,
-        ).wait_recv()
-
-    def c_copy(n, peer):
-        return pltpu.make_async_remote_copy(
-            s.at[n, rows(peer, 128)], h.at[n, rows(col, 128)], c_send.at[n, peer], c_recv.at[n, col],
-            device_id={"col": peer}, device_id_type=MESH,
-        )
-
-    def c_wait(n, peer):
-        pltpu.make_async_remote_copy(
-            s.at[n, rows(peer, 128)], h.at[n, rows(peer, 128)], c_send.at[n, peer], c_recv.at[n, peer],
-            device_id={"col": peer}, device_id_type=MESH,
-        ).wait_recv()
-
-    def each_col(do):
-        def step(d, _):
-            do(col_peer(d))
-            return 0
-
-        lax.fori_loop(1, COLS, step, 0)
-
-    def each_row(do):
-        def step(d, _):
-            do(row_peer(d))
-            return 0
-
-        lax.fori_loop(1, ROWS, step, 0)
-
-    each_col(lambda p: id_copy(p).start())
-    ids[col] = wanted[col]
-    vel_copy.wait()
-    each_col(id_wait)
+    wide = lax.broadcasted_iota(jnp.int32, (2 * TY, SLOTS * TY), 1)
+    deep = lax.broadcasted_iota(jnp.int32, (2 * TY, SLOTS * TY), 0)
+    for n in range(0, REQ, 2):
+        cell = jnp.where(deep < TY, slots[n] * TY + deep, slots[n + 1] * TY + deep - TY)
+        take[n * TY : (n + 2) * TY, :] = jnp.where(wide == cell, 1.0, 0.0).astype(BF16)
+    across = lax.broadcasted_iota(jnp.int32, (8, REQ * TY), 1)
+    cell = jnp.zeros((8, REQ * TY), jnp.int32)
+    for n in range(REQ):
+        cell = jnp.where(lax.shift_right_logical(across, 3) == n, slots[n] * TY, cell)
+    cell = jnp.broadcast_to((cell + (across & 7))[0:1], (128, REQ * TY))
+    down = lax.broadcasted_iota(jnp.int32, (128, REQ * TY), 0)
+
+    def build(i, _):
+        give[rows(i, 128), :] = jnp.where(down + i * 128 == cell, 1.0, 0.0).astype(BF16)
+        return 0
+
+    lax.fori_loop(0, SLOTS * TY // 128, build, 0)
+
+    hi, lo = split(table[...])
+    tab_h[...] = hi
+    tab_l[...] = lo
+    for i in range(16):
+        tw[i] = jnp.broadcast_to(tw_in[:, i : i + 1], (256, 128))
+
+    loads[4].wait()
+    id_all_copies().wait_recv()
     id_all = ids[...].reshape(SLOTS, 128)
-    lane = lax.broadcasted_iota(jnp.int32, (128, 128), 1)
     for j in range(4):
         hit = jnp.where(id_all == lane + 128 * j, 1.0, 0.0).astype(F32)
         at = slice(j * 128, (j + 1) * 128)
@@ -212,26 +252,8 @@
     gather(0)
     gather(1)
 
-    def select(at_ref, to, count, width):
-        def block(i, _):
-            at = rows(i, 128)
-            for j in range(width // 128):
-                hit = jnp.where(at_ref[at, :] == lane + 128 * j, 1.0, 0.0)
-                to[at, j * 128 : (j + 1) * 128] = hit.astype(BF16)
-            return 0
-
-        lax.fori_loop(0, count // 128, block, 0)
-
-    select(take_at, take, REQ * TY, SLOTS * TY)
-    select(give_at, give, SLOTS * TY, REQ * TY)
-
-    hi, lo = split(table[...])
-    tab_h[...] = hi
-    tab_l[...] = lo
-    for i in range(16):
-        tw[i] = jnp.broadcast_to(tw_in[:, i : i + 1], (256, 128))
-
-    zinv_copy.wait()
+    for load in loads[5:8] + loads[10:]:
+        load.wait()
 
     def cut(i, _):
         at = rows(i, 128)
@@ -244,12 +266,12 @@
     lax.fori_loop(0, 8, cut, 0)
 
     def markers(c):
-        each_col(lambda p: f_wait(c, p))
+        f_all(c).wait_recv()
         f_hi, f_lo = split(fr[c])
         mine = dot(take[...], f_hi) + dot(take[...], f_lo)
         for b in range(8):
-            at = slice(b * K * TY, (b + 1) * K * TY)
-            p_hi, p_lo = split(mine[at, :])
+            own = [slice((k * 8 + b) * TY, (k * 8 + b + 1) * TY) for k in range(K)]
+            p_hi, p_lo = split(jnp.concatenate([mine[at, :] for at in own], axis=0))
             inner = dot(p_hi, vth[b]) + (dot(p_lo, vth[b]) + dot(p_hi, vtl[b]))
             w = weight[b]
             sampled = jnp.sum(w * inner, axis=0, keepdims=True)
@@ -258,24 +280,26 @@
             s_hi, s_lo = split(w * (surf[b : b + 1, :] * force))
             last = ((1,), (1,))
             back = dot(s_hi, vth[b], last) + (dot(s_lo, vth[b], last) + dot(s_hi, vtl[b], last))
-            spread[at, :] = back
+            for k in range(K):
+                spread[own[k], :] = back[k * TY : (k + 1) * TY, :]
         b_hi, b_lo = split(spread[...])
         ro[c] = dot(give[...], b_hi) + dot(give[...], b_lo)
         each_col(lambda p: b_copy(c, p).start())
         ri[c, rows(col, 64), :] = ro[c, rows(col, 64), :]
 
+    def row_sends(n):
+        each_row(lambda p: r_copy(n, p).start())
+        g[n, rows(row, 256), :] = v[n // 2, r_rows(n, row), :]
+
     def force_tiles(c):
-        each_col(lambda p: b_wait(c, p))
+        b_all(c).wait_recv()
         for q in range(4):
             hi, lo = pair(ri, c, q, SLOTS)
             delta = dot(put[...], jnp.concatenate([hi, lo], axis=0))
             for e in range(2):
                 at = pl.ds(2 * q + e, TILES, stride=TY)
                 v[c, at, :] = v[c, at, :] + delta[:, e * 128 : (e + 1) * 128]
-        for e in range(2):
-            n = 2 * c + e
-            each_row(lambda p: r_copy(n, p).start())
-            g[n, row] = v[c, r_rows(n, row), :]
+        row_sends(c)
 
     def first(c, _):
         @pl.when(c < 3)
@@ -297,9 +321,14 @@
     low = lane < 64
 
     def axial(n):
-        each_row(lambda p: r_wait(n, p))
+        r_all(n).wait_recv()
+
+        @pl.when(n < 3)
+        def _():
+            row_sends(n + 3)
+
         for r in range(ROWS):
-            hi, lo = split(g[n, r])
+            hi, lo = split(g[n, r * 256 : (r + 1) * 256, :])
             xh[0:256, r * 128 : (r + 1) * 128] = hi
             xh[256:512, r * 128 : (r + 1) * 128] = lo
 
@@ -323,7 +352,7 @@
     half = np.float32(np.sqrt(0.5))
 
     def fourier(n):
-        each_col(lambda p: c_wait(n, p))
+        c_all(n).wait_recv()
         for q in range(4):
             a = h[n, pl.ds(2 * q, 256, stride=8), :]
             b = h[n, pl.ds(2 * q + 1, 256, stride=8), :]
@@ -386,40 +415,17 @@
 
     lax.fori_loop(0, CHUNKS + 1, second, 0)
 
-    each_col(lambda p: id_copy(p).wait_send())
-
-    def drain3(c, _):
-        each_col(lambda p: f_copy(c, p).wait_send())
-        each_col(lambda p: b_copy(c, p).wait_send())
-        return 0
-
-    def drain6(n, _):
-        each_row(lambda p: r_copy(n, p).wait_send())
-        each_col(lambda p: c_copy(n, p).wait_send())
+    id_all_copies().wait_send()
+    for c in range(3):
+        f_all(c).wait_send()
+        b_all(c).wait_send()
+    for n in range(CHUNKS):
+        r_all(n).wait_send()
+        c_all(n).wait_send()
         out_copy(n).wait()
-        return 0
-
-    lax.fori_loop(0, 3, drain3, 0)
-    lax.fori_loop(0, CHUNKS, drain6, 0)
 
 
 def local(velocity, z_inverse, tiles, amplitude, lateral, vertical, wall_velocity, surface):
-    wants = tiles.reshape(-1)
-    holder = wants // TILES
-    within = wants % TILES
-    order = jnp.arange(REQ, dtype=jnp.int32)
-    before = (holder[:, None] == holder[None, :]) & (order[None, :] < order[:, None])
-    slot_of = holder * CAP + jnp.sum(before.astype(jnp.int32), axis=1)
-    match = jnp.arange(SLOTS, dtype=jnp.int32)[:, None] == slot_of[None, :]
-    wanted = jnp.sum(jnp.where(match, within[None, :], 0), axis=1)
-    source = jnp.sum(jnp.where(match, order[None, :] - REQ, 0), axis=1) + REQ
-    wanted = jnp.broadcast_to(wanted[:, None], (SLOTS, 128)).reshape(COLS, CAP, 128)
-    line = jnp.arange(TY, dtype=jnp.int32)
-
-    def spread_out(index):
-        cells = index[:, None, None] * TY + line[None, :, None]
-        return jnp.broadcast_to(cells, (index.shape[0], TY, 128)).reshape(-1, 128)
-
     table, twiddle, damping = tables()
     any_ = pl.BlockSpec(memory_space=pl.ANY)
     vmem = pl.BlockSpec(memory_space=pltpu.VMEM)
@@ -430,9 +436,19 @@
             jax.ShapeDtypeStruct((2, 3, 2, 128, 1024), F32),
             jax.ShapeDtypeStruct((3, 8, 256), F32),
         ),
-        in_specs=[any_, any_] + [vmem] * 11,
+        in_specs=[any_] * 11,
         out_specs=(any_, vmem),
         scratch_shapes=[
+            pltpu.SMEM((4, 8), jnp.int32),
+            pltpu.VMEM((8, 4, 256), F32),
+            pltpu.VMEM((8, 8, 256), F32),
+            pltpu.VMEM((8, 128, 256), F32),
+            pltpu.VMEM((3, 8, 256), F32),
+            pltpu.VMEM((8, 256), F32),
+            pltpu.VMEM((512, 256), F32),
+            pltpu.VMEM((256, 128), F32),
+            pltpu.VMEM((1, 1024), F32),
+            pltpu.VMEM((COLS, CAP, 128), jnp.int32),
             pltpu.VMEM((3, 4096, 128), F32),
             pltpu.VMEM((1024, 1024), F32),
             pltpu.VMEM((4, 1024, 256), BF16),
@@ -453,28 +469,23 @@
             pltpu.VMEM((REQ * TY, 128), F32),
             pltpu.VMEM((3, SLOTS * TY, 128), F32),
             pltpu.VMEM((3, SLOTS * TY, 128), F32),
-            pltpu.VMEM((CHUNKS, ROWS, 256, 128), F32),
+            pltpu.VMEM((CHUNKS, ROWS * 256, 128), F32),
             pltpu.VMEM((512, 1024), BF16),
             pltpu.VMEM((CHUNKS, NY, 128), F32),
             pltpu.VMEM((CHUNKS, NY, 128), F32),
             pltpu.VMEM((8, 512, 128), F32),
             pltpu.VMEM((2, 4, 256, 128), F32),
             pltpu.VMEM((CHUNKS, 2, 128, 1024), F32),
-            dma((2,)),
-            dma((COLS,)), dma((COLS,)),
-            dma((3, COLS)), dma((3, COLS)),
-            dma((3, COLS)), dma((3, COLS)),
-            dma((CHUNKS, ROWS)), dma((CHUNKS, ROWS)),
-            dma((CHUNKS, COLS)), dma((CHUNKS, COLS)),
-            dma((CHUNKS,)),
+            dma((11,)), dma((1,)), dma((1,)),
+            dma((3,)), dma((3,)), dma((3,)), dma((3,)),
+            dma((CHUNKS,)), dma((CHUNKS,)), dma((CHUNKS,)), dma((CHUNKS,)), dma((CHUNKS,)),
         ],
         compiler_params=pltpu.CompilerParams(
             collective_id=0, has_side_effects=True, vmem_limit_bytes=60 * 1024 * 1024
         ),
         name="slab",
     )(
-        velocity.reshape(3, 4096, 128), z_inverse, wanted, spread_out(slot_of), spread_out(source),
-        amplitude, lateral, vertical, wall_velocity.transpose(1, 0, 2), surface,
+        velocity.reshape(3, 4096, 128), z_inverse, tiles.T, amplitude, lateral, vertical, wall_velocity.transpose(1, 0, 2), surface,
         jnp.asarray(table), jnp.asarray(twiddle), jnp.asarray(damping),
     )
     return (spectrum.reshape(2, 3, 4, 64, 1024), force.transpose(1, 0, 2))

time: 158 us -> 142 us (0.90); the launches traced: 158 us -> 139 us
  Pallas kernels: 146 us -> 131 us
  local copies, waits for them, and re-layouts: 10.8 us -> 7.23 us
    pallas_call x1, Pallas kernels: 146 us -> 131 us  [local(): pl.pallas_call(kernel, out_shape=(jax.ShapeDtypeStruct((2, 3, 2, 128, 102...]
    broadcast_in_dim x4 -> x0, local copies, waits for them, and re-layouts: 2.52 us -> none  [the longest x2 1.74 us: spread_out(): return jnp.broadcast_to(cells, (index.shape[0], TY, 128)).reshape(-1, 128)]
    unnamed x5 -> x4, local copies, waits for them, and re-layouts: 7.99 us -> 7.23 us
where the time goes in v2:
time: 142 us; the launch traced here: 139 us
  Pallas kernels  131 us (92%)
  local copies, waits for them, and re-layouts  7.23 us (5%)
    pallas_call x1, Pallas kernels, local(): pl.pallas_call(kernel, out_shape=(jax.ShapeDtypeStruct((2, 3, 2, 128, 102...  131 us
    unnamed x4, local copies, waits for them, and re-layouts  7.23 us

profile of v2, /device:TPU:1, one launch (start us, length us, event | category | flops | bytes accessed | tf_op | source)
XLA Modules:
  0.0 139.3 jit_solution(8413688036542833599)
XLA Ops:
  0.6 131.4 %slab.1 = (f32[2,3,2,128,1024]{4,3,2,1,0:T(8,128)}, f32[3,8,256]{2,1,0:T(8,128)}) custom-call(f32[3,4096,128]{2,1,0:T(8,128)} %bitcast.5, f32[1024,1024]{1,0:T(8,128)} %zinv.1, s32[4,8]{1,0:T(4,128)} %bitcast.9, f32[8,4,256]{2,1,0:T(4,128)} %amp_in.1, f32[8,8,256]{2,1,0:T(8,128)} %lat_in.1, f32[8,128,256]{2,1,0:T(8,128)} %vert_in.1, f32[3,8,256]{2,1,0:T(8,128)} %bitcast.7, ...), custom_call_target="tpu_custom_call" | custom-call | tf_op jit(solution)/shard_map/slab/pallas_call | solution.py:433
  132.0 0.0 copy-start
  132.0 6.6 %copy.15 = f32[2,3,4,64,1024]{4,3,2,1,0:T(8,128)} copy(f32[2,3,4,64,1024]{4,3,2,1,0:T(8,128)} %bitcast.6) | data formatting | bytes 12582912
  138.7 0.0 copy-done
  138.7 0.6 copy.16
Async XLA Ops:
  132.0 6.6 %copy-start = (f32[3,8,256]{2,1,0:T(8,128)S(1)}, f32[3,8,256]{2,1,0:T(8,128)}, u32[]{:S(2)}) copy-start(f32[3,8,256]{2,1,0:T(8,128)} %get-tuple-element.5) | copy-start | bytes 73732

commit v3 on v2

--- a/solution.py
+++ b/solution.py
@@ -55,9 +55,9 @@
     out, force_out,
     tiles, amp, lat, vert, wall, surf, table, tw_in, damp, wanted,
     v, zf, zh, zl, vth, vtl, weight, tab_h, tab_l, tw, ids, pick, put, take, give,
-    fo, fr, spread, ro, ri, g, xh, s, h, u, xk, ob,
+    fo, fr, spread, ro, ri, g, xh, s, h, u, xk,
     load_sem, id_send, id_recv, f_send, f_recv, b_send, b_recv,
-    r_send, r_recv, c_send, c_recv, o_sem,
+    r_send, r_recv, c_send, c_recv,
 ):
     row = lax.axis_index("row")
     col = lax.axis_index("col")
@@ -231,9 +231,6 @@
         hit = jnp.where(id_all == lane + 128 * j, 1.0, 0.0).astype(F32)
         at = slice(j * 128, (j + 1) * 128)
         pick[:, at] = hit.astype(BF16)
-        hit = hit.T.astype(BF16)
-        put[at, 0:128] = hit
-        put[at, 128:256] = hit
 
     def pair(ref, c, q, n):
         a = ref[c, pl.ds(2 * q, n, stride=TY), :]
@@ -251,6 +248,11 @@
 
     gather(0)
     gather(1)
+    for j in range(4):
+        hit = jnp.where(id_all == lane + 128 * j, 1.0, 0.0).astype(F32).T.astype(BF16)
+        at = slice(j * 128, (j + 1) * 128)
+        put[at, 0:128] = hit
+        put[at, 128:256] = hit
 
     for load in loads[5:8] + loads[10:]:
         load.wait()
@@ -299,40 +301,24 @@
             for e in range(2):
                 at = pl.ds(2 * q + e, TILES, stride=TY)
                 v[c, at, :] = v[c, at, :] + delta[:, e * 128 : (e + 1) * 128]
-        row_sends(c)
-
-    def first(c, _):
-        @pl.when(c < 3)
-        def _():
-            markers(c)
-
-        @pl.when(c == 0)
-        def _():
-            gather(2)
-
-        @pl.when(c > 0)
-        def _():
-            force_tiles(c - 1)
-
-        return 0
-
-    lax.fori_loop(0, 4, first, 0)
+        pl.when(c < 2)(lambda: row_sends(c))
 
     low = lane < 64
 
     def axial(n):
         r_all(n).wait_recv()
 
-        @pl.when(n < 3)
-        def _():
-            row_sends(n + 3)
+        @pl.when(n == 1)
+        def _():
+            row_sends(2)
 
         for r in range(ROWS):
             hi, lo = split(g[n, r * 256 : (r + 1) * 256, :])
             xh[0:256, r * 128 : (r + 1) * 128] = hi
             xh[256:512, r * 128 : (r + 1) * 128] = lo
 
-        def tile(j, _):
+        def tile(turn, _):
+            j = lax.rem(z + turn, 4)
             acc = dot(xh[...], zh[j])
             acc = acc[0:256] + (acc[256:512] + dot(xh[0:256, :], zl[j]))
             for t in range(2):
@@ -340,14 +326,23 @@
                 a1 = acc[128:256, t * 128 : (t + 1) * 128]
                 s[n, rows(4 * j + 2 * t, 128), :] = jnp.where(low, a0, pltpu.roll(a1, 64, 1))
                 s[n, rows(4 * j + 2 * t + 1, 128), :] = jnp.where(low, pltpu.roll(a0, 64, 1), a1)
+
+            def send(d, _):
+                @pl.when(4 * turn + d > 0)
+                def _():
+                    c_copy(n, 4 * j + lax.rem(y + d, 4)).start()
+
+                return 0
+
+            lax.fori_loop(0, 4, send, 0)
             return 0
 
         lax.fori_loop(0, 4, tile, 0)
-        each_col(lambda p: c_copy(n, p).start())
         h[n, rows(col, 128), :] = s[n, rows(col, 128), :]
 
-    def out_copy(n):
-        return pltpu.make_async_copy(ob.at[n], out.at[:, n // 2, lax.rem(n, 2)], o_sem.at[n])
+        @pl.when((n > 0) & (n < 4))
+        def _():
+            row_sends(n + 2)
 
     half = np.float32(np.sqrt(0.5))
 
@@ -399,21 +394,32 @@
         for p in range(2):
             for k2 in range(4):
                 at = slice(k2 * 256, (k2 + 1) * 256)
-                ob[n, p, :, at] = xk[p, k2].T * damp[:, at]
-        out_copy(n).start()
-
-    def second(n, _):
-        @pl.when(n < CHUNKS)
-        def _():
-            axial(n)
-
-        @pl.when(n > 0)
-        def _():
-            fourier(n - 1)
+                out[p, n // 2, lax.rem(n, 2), :, at] = xk[p, k2].T * damp[:, at]
+
+    def step(i, _):
+        @pl.when(i < 3)
+        def _():
+            markers(i)
+
+        @pl.when(i == 0)
+        def _():
+            gather(2)
+
+        @pl.when((i > 2) & (i < 3 + CHUNKS))
+        def _():
+            axial(i - 3)
+
+        @pl.when((i > 0) & (i < 4))
+        def _():
+            force_tiles(i - 1)
+
+        @pl.when(i > 3)
+        def _():
+            fourier(i - 4)
 
         return 0
 
-    lax.fori_loop(0, CHUNKS + 1, second, 0)
+    lax.fori_loop(0, CHUNKS + 4, step, 0)
 
     id_all_copies().wait_send()
     for c in range(3):
@@ -422,7 +428,6 @@
     for n in range(CHUNKS):
         r_all(n).wait_send()
         c_all(n).wait_send()
-        out_copy(n).wait()
 
 
 def local(velocity, z_inverse, tiles, amplitude, lateral, vertical, wall_velocity, surface):
@@ -433,11 +438,11 @@
     spectrum, force = pl.pallas_call(
         kernel,
         out_shape=(
-            jax.ShapeDtypeStruct((2, 3, 2, 128, 1024), F32),
-            jax.ShapeDtypeStruct((3, 8, 256), F32),
+            pltpu.VMEM((2, 3, 2, 128, 1024), F32),
+            pltpu.VMEM((3, 8, 256), F32),
         ),
         in_specs=[any_] * 11,
-        out_specs=(any_, vmem),
+        out_specs=(vmem, vmem),
         scratch_shapes=[
             pltpu.SMEM((4, 8), jnp.int32),
             pltpu.VMEM((8, 4, 256), F32),
@@ -475,13 +480,12 @@
             pltpu.VMEM((CHUNKS, NY, 128), F32),
             pltpu.VMEM((8, 512, 128), F32),
             pltpu.VMEM((2, 4, 256, 128), F32),
-            pltpu.VMEM((CHUNKS, 2, 128, 1024), F32),
             dma((11,)), dma((1,)), dma((1,)),
             dma((3,)), dma((3,)), dma((3,)), dma((3,)),
-            dma((CHUNKS,)), dma((CHUNKS,)), dma((CHUNKS,)), dma((CHUNKS,)), dma((CHUNKS,)),
+            dma((CHUNKS,)), dma((CHUNKS,)), dma((CHUNKS,)), dma((CHUNKS,)),
         ],
         compiler_params=pltpu.CompilerParams(
-            collective_id=0, has_side_effects=True, vmem_limit_bytes=60 * 1024 * 1024
+            collective_id=0, has_side_effects=True, vmem_limit_bytes=53 * 1024 * 1024
         ),
         name="slab",
     )(

time: 142 us -> 132 us (0.930); the launches traced: 139 us -> 132 us
  local copies, waits for them, and re-layouts: 7.23 us -> 3.31 us
  Pallas kernels: 131 us -> 128 us
    unnamed x4 -> x2, local copies, waits for them, and re-layouts: 7.23 us -> 3.31 us
    pallas_call x1, Pallas kernels: 131 us -> 128 us  [local(): pl.pallas_call(kernel, out_shape=(pltpu.VMEM((2, 3, 2, 128, 1024), F32),...]
where the time goes in v3:
time: 132 us
  Pallas kernels  128 us (97%)
  local copies, waits for them, and re-layouts  3.31 us (3%)
    pallas_call x1, Pallas kernels, local(): pl.pallas_call(kernel, out_shape=(pltpu.VMEM((2, 3, 2, 128, 1024), F32),...  128 us
    unnamed x2, local copies, waits for them, and re-layouts  3.31 us

profile of v3, /device:TPU:1, one launch (start us, length us, event | category | flops | bytes accessed | tf_op | source)
XLA Modules:
  0.0 132.1 jit_solution(1204453353580099232)
XLA Ops:
  0.6 128.1 %slab.1 = (f32[2,3,2,128,1024]{4,3,2,1,0:T(8,128)S(1)}, f32[3,8,256]{2,1,0:T(8,128)S(1)}) custom-call(f32[3,4096,128]{2,1,0:T(8,128)} %bitcast.7, f32[1024,1024]{1,0:T(8,128)} %zinv.1, s32[4,8]{1,0:T(4,128)} %bitcast.9, f32[8,4,256]{2,1,0:T(4,128)} %amp_in.1, f32[8,8,256]{2,1,0:T(8,128)} %lat_in.1, f32[8,128,256]{2,1,0:T(8,128)} %vert_in.1, ...), custom_call_target="tpu_custom_call" | custom-call | tf_op jit(solution)/shard_map/slab/pallas_call | solution.py:438
  128.8 2.7 %copy.15 = f32[2,3,4,64,1024]{4,3,2,1,0:T(8,128)} copy(f32[2,3,4,64,1024]{4,3,2,1,0:T(8,128)S(1)} %bitcast.5) | data formatting | bytes 12582912
  131.5 0.6 copy.16
